TPU v7x, 128 devices: a whole 4x4x4 slice. The times are simulated.
128 devices in a mesh: zone: 8 (over x, y_lo), dev: 16 (over y_hi, z, core).
Axes of the slice: x: 4, y: 4 (y_hi: 2, y_lo: 2; y = y_hi * 2 + y_lo), z: 4, core: 2. Of those that a mesh axis runs over, the one named last changes fastest.
Arguments:
- node_features: bfloat16 [65536, 512], P(('zone', 'dev')), may hold values from -9 to 9
- neighbour_blocks: int32 [512, 32], P(('zone', 'dev')), may hold values from 0 to 511, as said below
- neighbour_count: int32 [512], P(('zone', 'dev')), may hold values from 8 to 32, as said below
- tile_valid: int32 [512], replicated, may hold values from 64 to 128
- w_query: bfloat16 [512, 512], replicated, may hold values from -0.5 to 0.5
- w_key: bfloat16 [512, 512], replicated, may hold values from -0.5 to 0.5
- w_value: bfloat16 [512, 512], replicated, may hold values from -0.25 to 0.25
- w_out: bfloat16 [512, 512], replicated, may hold values from -0.25 to 0.25
- w_gate: bfloat16 [512, 2048], replicated, may hold values from -0.25 to 0.25
- w_up: bfloat16 [512, 2048], replicated, may hold values from -0.25 to 0.25
- w_down: bfloat16 [2048, 512], replicated, may hold values from -0.125 to 0.125
Outputs:
- layer_out: bfloat16 [65536, 512], P(('zone', 'dev'))
Inputs may be any that keep to these rules, and one draw needn't show every extreme that they name: `neighbour_blocks`: each row lists 32 different blocks. Zones are runs of 64 blocks (zone of block g is g // 64); every listed block lies in the query block's zone or in one of the two zones beside it, counting around the last zone to the first. Each value is 8, 16 or 32, one value for each patch of 16 consecutive blocks (patch of block g is g // 16); only the first neighbour_count[b] slots of row b count.
All inputs are finite; a program needn't handle non-finite values.
Results may differ from a plain program's by a relative error of at most 0.007.
The roundings to bfloat16 on the way count: a program that leaves them out, or rounds other values in their place, can miss the bound.
Values may be sent and summed in bfloat16 or wider, within the bound.
A program may use at most 448 MiB of HBM per device.

v0:
```python
import math

import jax
import jax.numpy as jnp
from jax import lax
from jax.sharding import PartitionSpec as P

D = 512
HEADS = 4
TILE = 128
NB = 32


def padded(cells, sides, width):
    for axis, dim in sides:
        count = lax.axis_size(axis)
        head = lax.slice_in_dim(cells, 0, width, axis=dim)
        tail = lax.slice_in_dim(cells, cells.shape[dim] - width, cells.shape[dim], axis=dim)
        cells = jnp.concatenate(
            [
                lax.ppermute(tail, axis, [(i, (i + 1) % count) for i in range(count)]),
                cells,
                lax.ppermute(head, axis, [((i + 1) % count, i) for i in range(count)]),
            ],
            axis=dim,
        )
    return cells


def lookup_valid(block_ids, tile_valid):
    block_index = jnp.arange(tile_valid.shape[0], dtype=jnp.int32)
    matches = block_ids[..., None] == block_index
    return jnp.sum(jnp.where(matches, tile_valid, 0), axis=-1)


def finish_layer(node_features, attended, w_out, w_gate, w_up, w_down):
    residual = node_features.astype(jnp.float32) + jnp.dot(
        attended, w_out, preferred_element_type=jnp.float32
    )
    inverse = lax.rsqrt(jnp.mean(residual * residual, axis=-1, keepdims=True) + 1e-06)
    normed = (residual * inverse).astype(jnp.bfloat16)
    gate_part = jnp.dot(normed, w_gate, preferred_element_type=jnp.float32)
    up_part = jnp.dot(normed, w_up, preferred_element_type=jnp.float32)
    hidden = (jax.nn.silu(gate_part) * up_part).astype(jnp.bfloat16)
    return (residual + jnp.dot(hidden, w_down, preferred_element_type=jnp.float32)).astype(
        jnp.bfloat16
    )


def body(
    node_features,
    neighbour_blocks,
    neighbour_count,
    tile_valid,
    w_query,
    w_key,
    w_value,
    w_out,
    w_gate,
    w_up,
    w_down,
):
    local_rows = node_features.shape[0]
    local_blocks = local_rows // TILE
    head_dim = D // HEADS
    score_scale = 1.0 / math.sqrt(head_dim)
    zone_count = lax.axis_size("zone")
    zone_blocks = local_blocks * lax.axis_size("dev")
    zone_index = lax.axis_index("zone")
    queries = jnp.dot(node_features, w_query, preferred_element_type=jnp.float32).astype(
        jnp.bfloat16
    )
    queries = queries.reshape(local_blocks, TILE, HEADS, head_dim)
    payload_width = node_features.shape[1]
    home_zone = neighbour_blocks // zone_blocks
    relative = (home_zone - zone_index + 1) % zone_count
    candidate = relative * zone_blocks + neighbour_blocks % zone_blocks
    slot_live = jnp.arange(NB, dtype=jnp.int32)[None, :] < neighbour_count[:, None]
    row_index = jnp.arange(TILE, dtype=jnp.int32)
    sides = padded(node_features, (("zone", 0),), local_rows)
    near_rows = lax.all_gather(
        sides.reshape(3, local_rows, payload_width), "dev", axis=1, tiled=True
    )
    near_tiles = near_rows.reshape(3 * zone_blocks, TILE, payload_width)
    picked = jnp.take(near_tiles, candidate.reshape(-1), axis=0)
    shipped = picked.reshape(-1, payload_width)
    key_part = jnp.dot(shipped, w_key, preferred_element_type=jnp.float32).astype(jnp.bfloat16)
    value_part = jnp.dot(shipped, w_value, preferred_element_type=jnp.float32).astype(jnp.bfloat16)
    key_rows = key_part
    value_rows = value_part
    key_rows = key_rows.reshape(local_blocks, NB * TILE, HEADS, head_dim)
    value_rows = value_rows.reshape(local_blocks, NB * TILE, HEADS, head_dim)
    valid_rows = lookup_valid(neighbour_blocks, tile_valid)
    key_live = slot_live[:, :, None] & (row_index[None, None, :] < valid_rows[:, :, None])
    key_mask = key_live.reshape(local_blocks, 1, 1, NB * TILE)
    scores = (
        jnp.einsum("bqhd,bkhd->bhqk", queries, key_rows, preferred_element_type=jnp.float32)
        * score_scale
    )
    peak = jnp.max(jnp.where(key_mask, scores, -1e30), axis=-1, keepdims=True)
    weights = jnp.where(key_mask, jnp.exp(scores - peak), 0.0)
    denominator = jnp.sum(weights, axis=-1)
    summed = jnp.einsum(
        "bhqk,bkhd->bqhd",
        weights.astype(jnp.bfloat16),
        value_rows,
        preferred_element_type=jnp.float32,
    )
    attended = (
        (summed / jnp.transpose(denominator, (0, 2, 1))[..., None])
        .reshape(local_rows, D)
        .astype(jnp.bfloat16)
    )
    return finish_layer(node_features, attended, w_out, w_gate, w_up, w_down)


def solution(mesh):
    placed = (
        P(("zone", "dev"), None),
        P(("zone", "dev"), None),
        P(("zone", "dev")),
        P(),
        P(),
        P(),
        P(),
        P(),
        P(),
        P(),
        P(),
    )
    return jax.shard_map(
        body, mesh=mesh, in_specs=placed, out_specs=P(("zone", "dev"), None), check_vma=False
    )
```

profile of v0, /device:TPU:1, one launch (start us, length us, event | category | flops | bytes accessed | tf_op | source)
XLA Modules:
  0.0 387.4 jit_solution(8792942089422113987)
XLA Ops:
  6.5 0.0 copy-start
  6.5 0.0 all-gather.2.cloned.1.call-start
  6.5 2.1 collective-permute-start
  8.7 2.2 collective-permute-start.1
  10.9 20.0 %collective-permute-done = bf16[512,512]{1,0:T(8,128)(2,1)S(1)} collective-permute-done((bf16[512,512]{1,0:T(8,128)(2,1)}, bf16[512,512]{1,0:T(8,128)(2,1)S(1)}, u32[]{:S(2)}, u32[]{:S(2)}) %collective-permute-start) | collective-permute-done | bytes 524320 | tf_op jit(solution)/shard_map/ppermute | solution.py:21
  30.8 2.4 collective-permute-done.1
  33.2 2.4 pad_maximum_fusion
  35.6 0.0 all-gather.2.cloned.1.call-update
  35.6 0.7 fusion.43
  36.3 0.1 reshape.117
  36.4 0.1 reshape.114
  36.5 2.0 copy.25
  38.5 1.6 convolution_convert_fusion.2
  40.2 0.1 reshape.119
  40.3 0.9 select_reduce_fusion.1
  41.3 0.7 iota_compare_fusion.1
  42.0 0.1 broadcast_bitcast_fusion.1
  42.1 0.1 broadcast_bitcast_fusion
  42.2 0.1 broadcast_bitcast_fusion.2
  42.3 0.1 fusion.38
  42.3 143.6 %all-gather.2.cloned.1.call-done = bf16[3,8192,512]{2,1,0:T(8,128)(2,1)} async-done(((bf16[3,512,512]{2,1,0:T(8,128)(2,1)}), bf16[3,8192,512]{2,1,0:T(8,128)(2,1)}) %all-gather.2.cloned.1.call-update) | async-done | bytes 25165840 | tf_op jit(solution)/shard_map/all_gather | solution.py:81
  186.0 16.5 %gather_fusion = bf16[128,128,512]{2,1,0:T(8,128)(2,1)} fusion(bf16[192,128,512]{2,1,0:T(8,128)(2,1)} %bitcast.45, s32[1024]{0:T(1024)S(1)} %pad_clamp_fusion), kind=kCustom, calls=%fused_computation | custom fusion | bytes 33554944 | tf_op jit(solution)/shard_map/jit(_take)/gather | solution.py:85
  202.5 0.0 copy-start.1
  202.5 14.5 %bitcast_select_fusion = bf16[16384,512]{1,0:T(8,128)(2,1)} fusion(bf16[128,128,512]{2,1,0:T(8,128)(2,1)} %gather_fusion, pred[16384]{0:T(1024)(128)(4,1)S(1)} %broadcast_bitcast_fusion.2), kind=kLoop, calls=%fused_computation.8 | loop fusion | flops 8388608 | bytes 33570816 | tf_op jit(solution)/shard_map/jit(_take)/select_n | solution.py:85
  216.9 0.0 copy-done.1
  217.0 18.2 %convolution_convert_fusion = bf16[16384,512]{1,0:T(8,128)(2,1)} fusion(bf16[16384,512]{1,0:T(8,128)(2,1)} %bitcast_select_fusion, bf16[512,512]{1,0:T(8,128)(2,1)S(1)} %copy-done.1), kind=kOutput, calls=%fused_computation.6 | convolution fusion | flops 8598323200 | bytes 34078720 | tf_op jit(solution)/shard_map/dot_general | solution.py:87
  235.2 0.0 copy-start.2
  235.2 23.8 %reshape.120 = bf16[4,4096,4,128]{3,2,1,0:T(4,128)(2,1)} reshape(bf16[16384,512]{1,0:T(8,128)(2,1)} %convolution_convert_fusion) | data formatting | bytes 33554432 | tf_op jit(solution)/shard_map/reshape | solution.py:91
  259.0 0.0 copy-done.2
  259.0 18.2 %convolution_convert_fusion.1 = bf16[16384,512]{1,0:T(8,128)(2,1)} fusion(bf16[16384,512]{1,0:T(8,128)(2,1)} %bitcast_select_fusion, bf16[512,512]{1,0:T(8,128)(2,1)S(1)} %copy-done.2), kind=kOutput, calls=%fused_computation.7 | convolution fusion | flops 8598323200 | bytes 34078720 | tf_op jit(solution)/shard_map/dot_general | solution.py:88
  277.2 23.7 %reshape.118 = bf16[4,4096,4,128]{3,2,1,0:T(4,128)(2,1)} reshape(bf16[16384,512]{1,0:T(8,128)(2,1)} %convolution_convert_fusion.1) | data formatting | bytes 33554432 | tf_op jit(solution)/shard_map/reshape | solution.py:92
  300.9 18.3 %fusion.7 = f32[4,4,128,4096]{3,2,1,0:T(8,128)} fusion(bf16[4,4096,4,128]{3,2,1,0:T(4,128)(2,1)} %reshape.120, bf16[4,128,4,128]{3,2,1,0:T(4,128)(2,1)S(1)} %reshape.119), kind=kOutput, calls=%fused_computation.11 | convolution fusion | flops 2147483648 | bytes 50855936 | tf_op jit(solution)/shard_map/bqhd,bkhd->bhqk/dot_general | solution.py:97
  319.3 32.1 %fusion.49 = (f32[4,4,128]{2,1,0:T(4,128)S(1)}, bf16[4,4,128,4096]{3,2,1,0:T(8,128)(2,1)}) fusion(f32[4,4,128,4096]{3,2,1,0:T(8,128)} %fusion.7, pred[4,4096]{1,0:T(4,128)(4,1)S(1)} %fusion.38), kind=kOutput, calls=%fused_computation.68 | output fusion | flops 58724352 | bytes 50356224 | tf_op jit(solution)/shard_map/sub | solution.py:101
  351.4 13.8 %fusion.26 = bf16[4,128,4,128]{1,3,2,0:T(8,128)(2,1)S(1)} fusion(bf16[4,4,128,4096]{3,2,1,0:T(8,128)(2,1)} %get-tuple-element.6, bf16[4,4096,4,128]{3,2,1,0:T(4,128)(2,1)} %reshape.118, f32[4,128,4]{1,2,0:T(4,128)S(1)} %bitcast.48), kind=kOutput, calls=%fused_computation.26 | convolution fusion | flops 2148007936 | bytes 34086912 | tf_op jit(solution)/shard_map/bhqk,bkhd->bqhd/dot_general | solution.py:103
  365.2 1.1 copy.29
  366.3 1.9 multiply_reduce_fusion
  368.2 0.0 copy-done
  368.2 3.2 fusion.31
  371.4 7.1 %fusion.25 = bf16[512,512]{0,1:T(8,128)(2,1)} fusion(f32[512,512]{0,1:T(8,128)S(1)} %get-tuple-element.8, bf16[2048,512]{1,0:T(8,128)(2,1)} %param.21, f32[512,2048]{1,0:T(8,128)} %fusion.31, bf16[512,2048]{1,0:T(8,128)(2,1)} %param.20, f32[512]{0:T(512)S(1)} %add_rsqrt_fusion), kind=kOutput, calls=%fused_computation.24 | convolution fusion | flops 2154823680 | bytes 9963520 | tf_op jit(solution)/shard_map/dot_general | solution.py:45
  378.5 2.0 copy.31
  (5 shorter events, 0.0 us)
Async XLA Ops:
  6.5 361.6 %copy-start = (bf16[512,2048]{1,0:T(8,128)(2,1)S(1)}, bf16[512,2048]{1,0:T(8,128)(2,1)}, u32[]{:S(2)}) copy-start(bf16[512,2048]{1,0:T(8,128)(2,1)} %param.19) | copy-start | bytes 6291460
  6.5 179.4 %all-gather.2.cloned.1.call-start = ((), (), s32[]{:S(2)}) async-start(), calls=%async_computation | async-start | bytes 26738688 | tf_op jit(solution)/shard_map/all_gather | solution.py:81
  6.5 24.3 %collective-permute-start = (bf16[512,512]{1,0:T(8,128)(2,1)}, bf16[512,512]{1,0:T(8,128)(2,1)S(1)}, u32[]{:S(2)}, u32[]{:S(2)}) collective-permute-start(bf16[512,512]{1,0:T(8,128)(2,1)} %param.11), channel_id=1, source_target_pairs={{0,16},{16,32},{32,48},{48,64},{64,80},{80,96},{96,112},{112,0},{1... | collective-permute-start | bytes 1572872 | tf_op jit(solution)/shard_map/ppermute | solution.py:21
  8.7 24.6 %collective-permute-start.1 = (bf16[512,512]{1,0:T(8,128)(2,1)}, bf16[512,512]{1,0:T(8,128)(2,1)S(1)}, u32[]{:S(2)}, u32[]{:S(2)}) collective-permute-start(bf16[512,512]{1,0:T(8,128)(2,1)} %param.11), channel_id=1, source_target_pairs={{16,0},{32,16},{48,32},{64,48},{80,64},{96,80},{112,96},{0,112},{1... | collective-permute-start | bytes 1572872 | tf_op jit(solution)/shard_map/ppermute | solution.py:23
  202.5 14.5 %copy-start.1 = (bf16[512,512]{1,0:T(8,128)(2,1)S(1)}, bf16[512,512]{1,0:T(8,128)(2,1)}, u32[]{:S(2)}) copy-start(bf16[512,512]{1,0:T(8,128)(2,1)} %param.16) | copy-start | bytes 1572868
  235.2 23.8 %copy-start.2 = (bf16[512,512]{1,0:T(8,128)(2,1)S(1)}, bf16[512,512]{1,0:T(8,128)(2,1)}, u32[]{:S(2)}) copy-start(bf16[512,512]{1,0:T(8,128)(2,1)} %param.17) | copy-start | bytes 1572868
Sparse Core Ops, SparseCore 0:
  35.7 150.1 all-gather.1
where the time goes:
time: 389 us; the launch traced here: 387 us
  waiting for transfers between devices  166 us (43%)
  matrix products  82.4 us (21%)
  local copies, waits for them, and re-layouts  69.7 us (18%)
  other arithmetic  51.4 us (13%)
  between operations  13.5 us (3%)
  starting transfers between devices  4.31 us (1%)
    all_gather x1, waiting for transfers between devices, body(): lax.all_gather(sides.reshape(3, local_rows, payload_width), 'dev', axis=1...  144 us
    sub x1, other arithmetic, body(): weights = jnp.where(key_mask, jnp.exp(scores - peak), 0.0)  32.1 us
    reshape x1, local copies, waits for them, and re-layouts, body(): key_rows = key_rows.reshape(local_blocks, NB * TILE, HEADS, head_dim)  23.8 us
    reshape x1, local copies, waits for them, and re-layouts, body(): value_rows = value_rows.reshape(local_blocks, NB * TILE, HEADS, head_dim)  23.7 us
    ppermute x1, waiting for transfers between devices, padded(): lax.ppermute(tail, axis, [(i, (i + 1) % count) for i in range(count)])  20 us
    dot_general x1, matrix products, body(): jnp.einsum('bqhd,bkhd->bhqk', queries, key_rows, preferred_element_type=j...  18.3 us
    dot_general x1, matrix products, body(): jnp.dot(shipped, w_value, preferred_element_type=jnp.float32)  18.2 us
    dot_general x1, matrix products, body(): jnp.dot(shipped, w_key, preferred_element_type=jnp.float32)  18.2 us
  transfers between devices with their start and end apart: 3, of which 3 were waited for; matrix products, arithmetic and copies ran while one was open for 2% of the time, Pallas kernels for 0%

commit v1 on v0

v1 whole, which is shorter than its diff:
```python
import functools
import math

import jax
import jax.numpy as jnp
from jax import lax
from jax.experimental import pallas as pl
from jax.experimental.pallas import tpu as pltpu
from jax.sharding import PartitionSpec as P

D = 512
HEADS = 4
HD = 128
TILE = 128
NB = 32
ZD = 4
NEG = -1e30
EXP_SCALE = math.log2(math.e) / math.sqrt(HD)


def proj_kernel(x_ref, wq_ref, wk_ref, wv_ref, q_ref, kv_ref):
    def one_tile(t, carry):
        x = x_ref[pl.ds(pl.multiple_of(t * TILE, TILE), TILE), :]
        q = jnp.dot(x, wq_ref[...], preferred_element_type=jnp.float32).astype(jnp.bfloat16)
        for h in range(HEADS):
            q_ref[h, t] = q[:, h * HD:(h + 1) * HD]
        k = jnp.dot(x, wk_ref[...], preferred_element_type=jnp.float32)
        for h in range(HEADS):
            kv_ref[h, t, 0] = jnp.transpose(k[:, h * HD:(h + 1) * HD]).astype(jnp.bfloat16)
        v = jnp.dot(x, wv_ref[...], preferred_element_type=jnp.float32).astype(jnp.bfloat16)
        for h in range(HEADS):
            kv_ref[h, t, 1] = v[:, h * HD:(h + 1) * HD]
        return carry

    lax.fori_loop(0, x_ref.shape[0] // TILE, one_tile, 0)


def project(x, wq, wk, wv):
    tiles = x.shape[0] // TILE
    return pl.pallas_call(
        proj_kernel,
        out_shape=(
            jax.ShapeDtypeStruct((HEADS, tiles, TILE, HD), jnp.bfloat16),
            jax.ShapeDtypeStruct((HEADS, tiles, 2, TILE, HD), jnp.bfloat16),
        ),
    )(x, wq, wk, wv)


def attn_kernel(code_ref, q_ref, kv_hbm, o_ref, kv_ref, s_ref, sem):
    chunks = 6
    step = kv_hbm.shape[0] // chunks
    copies = [
        pltpu.make_async_copy(
            kv_hbm.at[pl.ds(i * step, step)], kv_ref.at[pl.ds(i * step, step)], sem.at[i]
        )
        for i in range(chunks)
    ]
    for c in copies:
        c.start()
    for c in copies:
        c.wait()
    lane = lax.broadcasted_iota(jnp.int32, (1, TILE), 1)

    def one_tile(i, carry):
        groups = code_ref[i, NB] // 8
        q = q_ref[i]

        def scores(c, top):
            for p in range(4):
                a = code_ref[i, c * 8 + 2 * p]
                b = code_ref[i, c * 8 + 2 * p + 1]
                keys = jnp.concatenate([kv_ref[a // 256, 0], kv_ref[b // 256, 0]], axis=1)
                s = jnp.dot(q, keys, preferred_element_type=jnp.float32)
                bias = jnp.concatenate(
                    [
                        jnp.where(lane < a % 256, 0.0, NEG),
                        jnp.where(lane < b % 256, 0.0, NEG),
                    ],
                    axis=1,
                )
                s = s + bias
                s_ref[c, :, p * 256:(p + 1) * 256] = s
                top = jnp.maximum(top, jnp.maximum(s[:, :TILE], s[:, TILE:]))
            return top

        top = lax.fori_loop(0, groups, scores, jnp.full((TILE, TILE), NEG, jnp.float32))
        peak = jnp.max(top, axis=1, keepdims=True)

        def values(c, state):
            den, acc = state
            ps, vs = [], []
            for p in range(4):
                a = code_ref[i, c * 8 + 2 * p]
                b = code_ref[i, c * 8 + 2 * p + 1]
                w = jnp.exp2((s_ref[c, :, p * 256:(p + 1) * 256] - peak) * EXP_SCALE)
                den = den + (w[:, :TILE] + w[:, TILE:])
                ps.append(w.astype(jnp.bfloat16))
                vs += [kv_ref[a // 256, 1], kv_ref[b // 256, 1]]
            acc = acc + jnp.dot(
                jnp.concatenate(ps, axis=1),
                jnp.concatenate(vs, axis=0),
                preferred_element_type=jnp.float32,
            )
            return den, acc

        zero = jnp.zeros((TILE, TILE), jnp.float32)
        den, acc = lax.fori_loop(0, groups, values, (zero, zero))
        o_ref[i] = (acc / jnp.sum(den, axis=1, keepdims=True)).astype(jnp.bfloat16)
        return carry

    lax.fori_loop(0, q_ref.shape[0], one_tile, 0)


def attend(code, q, kv):
    return pl.pallas_call(
        attn_kernel,
        out_shape=jax.ShapeDtypeStruct(q.shape, jnp.bfloat16),
        in_specs=[
            pl.BlockSpec(memory_space=pltpu.SMEM),
            pl.BlockSpec(memory_space=pltpu.VMEM),
            pl.BlockSpec(memory_space=pl.ANY),
        ],
        out_specs=pl.BlockSpec(memory_space=pltpu.VMEM),
        scratch_shapes=[
            pltpu.VMEM(kv.shape, jnp.bfloat16),
            pltpu.VMEM((4, TILE, 8 * TILE), jnp.float32),
            pltpu.SemaphoreType.DMA((6,)),
        ],
        compiler_params=pltpu.CompilerParams(vmem_limit_bytes=40 * 1024 * 1024),
    )(code, q, kv)


def finish_layer(node_features, attended, w_out, w_gate, w_up, w_down):
    residual = node_features.astype(jnp.float32) + jnp.dot(
        attended, w_out, preferred_element_type=jnp.float32
    )
    inverse = lax.rsqrt(jnp.mean(residual * residual, axis=-1, keepdims=True) + 1e-06)
    normed = (residual * inverse).astype(jnp.bfloat16)
    gate_part = jnp.dot(normed, w_gate, preferred_element_type=jnp.float32)
    up_part = jnp.dot(normed, w_up, preferred_element_type=jnp.float32)
    hidden = (jax.nn.silu(gate_part) * up_part).astype(jnp.bfloat16)
    return (residual + jnp.dot(hidden, w_down, preferred_element_type=jnp.float32)).astype(
        jnp.bfloat16
    )


def make_codes(neighbour_blocks, neighbour_count, tile_valid, zone_blocks, zone_count):
    zone_index = lax.axis_index("zone")
    relative = (neighbour_blocks // zone_blocks - zone_index + 1) % zone_count
    local = neighbour_blocks % zone_blocks
    y_hi, rest = local // 32, local % 32
    z, rest = rest // 8, rest % 8
    core, t = rest // 4, rest % 4
    slot = (((relative * 2 + y_hi) * 2 + core) * ZD + z) * 4 + t
    matches = neighbour_blocks[..., None] == jnp.arange(tile_valid.shape[0], dtype=jnp.int32)
    valid = jnp.sum(jnp.where(matches, tile_valid, 0), axis=-1)
    live = jnp.arange(NB, dtype=jnp.int32)[None, :] < neighbour_count[:, None]
    code = slot * 256 + jnp.where(live, valid, 0)
    return jnp.concatenate(
        [code, neighbour_count[:, None], jnp.zeros((code.shape[0], 95), jnp.int32)], axis=1
    )


def body(
    x,
    neighbour_blocks,
    neighbour_count,
    tile_valid,
    w_query,
    w_key,
    w_value,
    w_out,
    w_gate,
    w_up,
    w_down,
):
    rows = x.shape[0]
    tiles = rows // TILE
    zone_count = lax.axis_size("zone")
    dev_count = lax.axis_size("dev")
    z_groups = [
        [y * 8 + z * 2 + c for z in range(ZD)] for y in range(2) for c in range(2)
    ]
    plane_groups = [
        [y * 8 + z * 2 + c for y in range(2) for c in range(2)] for z in range(ZD)
    ]
    codes = make_codes(
        neighbour_blocks, neighbour_count, tile_valid, tiles * dev_count, zone_count
    )
    q, kv = project(x, w_query, w_key, w_value)
    codes = lax.all_gather(codes, "dev", axis=0, axis_index_groups=z_groups, tiled=True)
    q = lax.all_to_all(q, "dev", 0, 0, axis_index_groups=z_groups, tiled=True)
    kv = lax.all_to_all(kv, "dev", 0, 0, axis_index_groups=z_groups, tiled=True)
    own = lax.all_gather(kv, "dev", axis=0, axis_index_groups=plane_groups)
    own = own.reshape(dev_count * tiles, 2, TILE, HD)
    ring = [(i, (i + 1) % zone_count) for i in range(zone_count)]
    before = lax.ppermute(own, "zone", ring)
    after = lax.ppermute(own, "zone", [(b, a) for a, b in ring])
    near = jnp.concatenate([before, own, after], axis=0)
    o = attend(codes, q.reshape(ZD * tiles, TILE, HD), near)
    o = lax.all_to_all(
        o.reshape(ZD, tiles, TILE, HD), "dev", 0, 0, axis_index_groups=z_groups, tiled=True
    )
    attended = jnp.transpose(o, (1, 2, 0, 3)).reshape(rows, D)
    return finish_layer(x, attended, w_out, w_gate, w_up, w_down)


def solution(mesh):
    placed = (
        P(("zone", "dev"), None),
        P(("zone", "dev"), None),
        P(("zone", "dev")),
        P(),
        P(),
        P(),
        P(),
        P(),
        P(),
        P(),
        P(),
    )
    return jax.shard_map(
        body, mesh=mesh, in_specs=placed, out_specs=P(("zone", "dev"), None), check_vma=False
    )
```

time: 389 us -> 340 us (0.87)
  the two profiles are of different devices: /device:TPU:1 before, /device:TPU:28 now
where the time goes in v1:
time: 340 us; the launch traced here: 339 us
  waiting for transfers between devices  207 us (61%)
  Pallas kernels  41.9 us (12%)
  blocking collectives  33.8 us (10%)
  between operations  13.4 us (4%)
  other arithmetic  12 us (4%)
  matrix products  12 us (4%)
  starting transfers between devices  10.9 us (3%)
  local copies, waits for them, and re-layouts  8.22 us (2%)
    ppermute x1, waiting for transfers between devices, body(): before = lax.ppermute(own, 'zone', ring)  163 us
    pallas_call x1, Pallas kernels, attend(): pl.pallas_call(attn_kernel, out_shape=jax.ShapeDtypeStruct(q.shape, jnp.b...  37.7 us
    all_gather x1, waiting for transfers between devices, body(): own = lax.all_gather(kv, 'dev', axis=0, axis_index_groups=plane_groups)  36.3 us
    all_to_all x1, blocking collectives, body(): kv = lax.all_to_all(kv, 'dev', 0, 0, axis_index_groups=z_groups, tiled=True)  20.5 us
    all_gather x1, blocking collectives, body(): lax.all_gather(codes, 'dev', axis=0, axis_index_groups=z_groups, tiled=True)  13.3 us
    concatenate x1, other arithmetic, body(): near = jnp.concatenate([before, own, after], axis=0)  11.6 us
    all_to_all x1, waiting for transfers between devices, body(): lax.all_to_all(o.reshape(ZD, tiles, TILE, HD), 'dev', 0, 0, axis_index_gr...  8.02 us
    dot_general x1, matrix products, finish_layer(): jnp.dot(hidden, w_down, preferred_element_type=jnp.float32)  7.07 us
  transfers between devices with their start and end apart: 5, of which 3 were waited for; matrix products, arithmetic and copies ran while one was open for 4% of the time, Pallas kernels for 0%

profile of v1, /device:TPU:28, one launch (start us, length us, event | category | flops | bytes accessed | tf_op | source)
XLA Modules:
  0.0 339.1 jit_solution(8887364313781648087)
XLA Ops:
  6.5 0.0 copy-start
  6.5 0.0 copy-start.4
  6.5 0.0 copy-start.3
  6.5 0.0 copy-start.5
  6.5 0.0 all-gather.4.cloned.1.call-start
  6.6 4.2 %shard_map.109 = (bf16[4,4,128,128]{3,2,1,0:T(8,128)(2,1)}, bf16[4,4,2,128,128]{4,3,2,1,0:T(8,128)(2,1)}) custom-call(bf16[512,512]{1,0:T(8,128)(2,1)} %x_ref.1, bf16[512,512]{1,0:T(8,128)(2,1)} %wq_ref.1, bf16[512,512]{1,0:T(8,128)(2,1)} %wk_ref.1, bf16[512,512]{1,0:T(8,128)(2,1)} %wv_ref.1), custom_call_target="tpu_custom_call" | custom-call | tf_op jit(solution)/shard_map/pallas_call | solution.py:40
  10.8 20.5 %all_to_all.15 = bf16[4,4,2,128,128]{4,3,2,1,0:T(8,128)(2,1)} all-to-all(bf16[4,4,2,128,128]{4,3,2,1,0:T(8,128)(2,1)} %get-tuple-element.8), channel_id=1, replica_groups={{0,2,4,6},{1,3,5,7},{8,10,12,14},{9,11,13,15},{16,18,20,22},{17,19,21,2..., dimensions={0} | all-to-all | bytes 2097152 | tf_op jit(solution)/shard_map/all_to_all | solution.py:193
  31.3 0.0 all-gather.4.cloned.1.call-update
  31.3 36.3 %all-gather.4.cloned.1.call-done = bf16[16,4,2,128,128]{4,3,2,1,0:T(8,128)(2,1)} async-done(((bf16[4,4,2,128,128]{4,3,2,1,0:T(8,128)(2,1)}), bf16[16,4,2,128,128]{4,3,2,1,0:T(8,128)(2,1)}) %all-gather.4.cloned.1.call-update) | async-done | bytes 4194320 | tf_op jit(solution)/shard_map/all_gather | solution.py:194
  67.6 0.5 collective-permute-start
  68.1 1.5 collective-permute-start.1
  69.6 4.4 %all-to-all-start = ((bf16[4,4,128,128]{3,2,1,0:T(8,128)(2,1)}), bf16[4,4,128,128]{3,2,1,0:T(8,128)(2,1)S(1)}, u32[]{:S(2)}, u32[]{:S(2)}) async-start(bf16[4,4,128,128]{3,2,1,0:T(8,128)(2,1)} %get-tuple-element.7), calls=%async_computation | async-start | bytes 1048576 | tf_op jit(solution)/shard_map/all_to_all | solution.py:192
  74.0 0.0 copy-done.4
  74.0 0.1 copy.27
  74.1 0.1 pad.5.clone
  74.2 0.0 copy-done.3
  74.2 0.0 copy-done.5
  74.2 0.2 select_reduce_fusion
  74.4 0.1 select_add_fusion
  74.5 0.1 add_bitcast_fusion
  74.6 13.3 %all-gather.1 = s32[4,4,128]{2,1,0:T(4,128)S(1)} all-gather(s32[1,4,128]{2,1,0:T(4,128)S(1)} %add_bitcast_fusion), channel_id=1, replica_groups={{0,2,4,6},{1,3,5,7},{8,10,12,14},{9,11,13,15},{16,18,20,22},{17,19,21,2..., dimensions={0}, use_global_device_ids=true | all-gather | bytes 10240 | tf_op jit(solution)/shard_map/all_gather | solution.py:191
  87.9 162.6 %collective-permute-done = bf16[64,2,128,128]{3,2,1,0:T(8,128)(2,1)} collective-permute-done((bf16[64,2,128,128]{3,2,1,0:T(8,128)(2,1)}, bf16[64,2,128,128]{3,2,1,0:T(8,128)(2,1)}, u32[]{:S(2)}, u32[]{:S(2)}) %collective-permute-start) | collective-permute-done | bytes 4194336 | tf_op jit(solution)/shard_map/ppermute | solution.py:197
  250.5 0.0 collective-permute-done.1
  250.5 11.6 %pad_maximum_fusion.kv_hbm = bf16[192,2,128,128]{3,2,1,0:T(8,128)(2,1)} fusion(bf16[64,2,128,128]{3,2,1,0:T(8,128)(2,1)} %collective-permute-done.1, bf16[64,2,128,128]{3,2,1,0:T(8,128)(2,1)} %bitcast.23, bf16[64,2,128,128]{3,2,1,0:T(8,128)(2,1)} %collective-permute-done), kind=kLoop, calls=%fused_computation | loop fusion | flops 12582912 | bytes 25165824 | tf_op jit(solution)/shard_map/concatenate | solution.py:199
  262.1 0.0 all-to-all-done
  262.1 0.0 copy-start.1
  262.1 4.6 %copy-done.1 = bf16[192,2,128,128]{3,2,1,0:T(8,128)(2,1)S(1)} copy-done((bf16[192,2,128,128]{3,2,1,0:T(8,128)(2,1)S(1)}, bf16[192,2,128,128]{3,2,1,0:T(8,128)(2,1)}, u32[]{:S(2)}) %copy-start.1) | copy-done | bytes 12582936
  266.7 0.0 copy-start.2
  266.7 37.7 %shard_map.110 = bf16[16,128,128]{2,1,0:T(8,128)(2,1)} custom-call(s32[16,128]{1,0:T(8,128)S(1)} %bitcast.20, bf16[16,128,128]{2,1,0:T(8,128)(2,1)S(1)} %bitcast.19, bf16[192,2,128,128]{3,2,1,0:T(8,128)(2,1)S(1)} %copy-done.1), custom_call_target="tpu_custom_call" | custom-call | tf_op jit(solution)/shard_map/pallas_call | solution.py:115
  304.3 4.4 %all-to-all-start.2 = ((bf16[4,4,128,128]{3,2,1,0:T(8,128)(2,1)}), bf16[4,4,128,128]{3,2,1,0:T(8,128)(2,1)S(1)}, u32[]{:S(2)}, u32[]{:S(2)}) async-start(bf16[4,4,128,128]{3,2,1,0:T(8,128)(2,1)} %bitcast.5), calls=%async_computation.2 | async-start | bytes 1048576 | tf_op jit(solution)/shard_map/all_to_all | solution.py:201
  308.8 0.0 copy-done.2
  308.8 1.0 copy.26
  309.8 8.0 %all-to-all-done.2 = bf16[4,4,128,128]{3,2,1,0:T(8,128)(2,1)S(1)} async-done(((bf16[4,4,128,128]{3,2,1,0:T(8,128)(2,1)}), bf16[4,4,128,128]{3,2,1,0:T(8,128)(2,1)S(1)}, u32[]{:S(2)}, u32[]{:S(2)}) %all-to-all-start.2) | async-done | bytes 524320 | tf_op jit(solution)/shard_map/all_to_all | solution.py:201
  317.8 0.4 copy.28
  318.2 1.7 multiply_reduce_fusion
  319.9 0.0 copy-done
  319.9 3.2 fusion.3
  323.2 7.1 %fusion.2 = bf16[512,512]{0,1:T(8,128)(2,1)} fusion(f32[512,512]{0,1:T(8,128)S(1)} %get-tuple-element.10, bf16[2048,512]{1,0:T(8,128)(2,1)} %param.21, f32[512,2048]{1,0:T(8,128)} %fusion.3, bf16[512,2048]{1,0:T(8,128)(2,1)} %param.20, f32[512]{0:T(512)S(1)} %add_rsqrt_fusion), kind=kOutput, calls=%fused_computation.5 | convolution fusion | flops 2154823680 | bytes 9963520 | tf_op jit(solution)/shard_map/dot_general | solution.py:142
  330.3 2.0 copy.30
  (2 shorter events, 0.0 us)
Async XLA Ops:
  6.5 313.4 %copy-start = (bf16[512,2048]{1,0:T(8,128)(2,1)S(1)}, bf16[512,2048]{1,0:T(8,128)(2,1)}, u32[]{:S(2)}) copy-start(bf16[512,2048]{1,0:T(8,128)(2,1)} %param.19) | copy-start | bytes 6291460
  6.5 67.5 %copy-start.4 = (s32[4]{0:T(128)S(1)}, s32[4]{0:T(128)}, u32[]{:S(2)}) copy-start(s32[4]{0:T(128)} %param.13) | copy-start | bytes 52
  6.5 67.7 %copy-start.3 = (s32[4,32]{1,0:T(4,128)S(1)}, s32[4,32]{1,0:T(4,128)}, u32[]{:S(2)}) copy-start(s32[4,32]{1,0:T(4,128)} %param.12) | copy-start | bytes 1540
  6.5 67.7 %copy-start.5 = (s32[512]{0:T(512)S(1)}, s32[512]{0:T(512)}, u32[]{:S(2)}) copy-start(s32[512]{0:T(512)} %param.14) | copy-start | bytes 6148
  6.5 61.1 %all-gather.4.cloned.1.call-start = ((), (), s32[]{:S(2)}) async-start(), calls=%async_computation.3 | async-start | bytes 5242880 | tf_op jit(solution)/shard_map/all_gather | solution.py:194
  67.6 182.9 %collective-permute-start = (bf16[64,2,128,128]{3,2,1,0:T(8,128)(2,1)}, bf16[64,2,128,128]{3,2,1,0:T(8,128)(2,1)}, u32[]{:S(2)}, u32[]{:S(2)}) collective-permute-start(bf16[64,2,128,128]{3,2,1,0:T(8,128)(2,1)} %bitcast.21), channel_id=1, source_target_pairs={{0,16},{16,32},{32,48},{48,64},{64,80},{80,96},{96,112},{112,0},{1... | collective-permute-start | bytes 12582920 | tf_op jit(solution)/shard_map/ppermute | solution.py:197
  68.1 182.4 %collective-permute-start.1 = (bf16[64,2,128,128]{3,2,1,0:T(8,128)(2,1)}, bf16[64,2,128,128]{3,2,1,0:T(8,128)(2,1)}, u32[]{:S(2)}, u32[]{:S(2)}) collective-permute-start(bf16[64,2,128,128]{3,2,1,0:T(8,128)(2,1)} %bitcast.22), channel_id=1, source_target_pairs={{16,0},{32,16},{48,32},{64,48},{80,64},{96,80},{112,96},{0,112},{1... | collective-permute-start | bytes 12582920 | tf_op jit(solution)/shard_map/ppermute | solution.py:198
  69.6 192.5 %all-to-all-start = ((bf16[4,4,128,128]{3,2,1,0:T(8,128)(2,1)}), bf16[4,4,128,128]{3,2,1,0:T(8,128)(2,1)S(1)}, u32[]{:S(2)}, u32[]{:S(2)}) async-start(bf16[4,4,128,128]{3,2,1,0:T(8,128)(2,1)} %get-tuple-element.7), calls=%async_computation | async-start | bytes 1048576 | tf_op jit(solution)/shard_map/all_to_all | solution.py:192
  262.1 4.6 %copy-start.1 = (bf16[192,2,128,128]{3,2,1,0:T(8,128)(2,1)S(1)}, bf16[192,2,128,128]{3,2,1,0:T(8,128)(2,1)}, u32[]{:S(2)}) copy-start(bf16[192,2,128,128]{3,2,1,0:T(8,128)(2,1)} %pad_maximum_fusion.kv_hbm) | copy-start | bytes 37748740
  266.7 42.1 %copy-start.2 = (bf16[512,512]{1,0:T(8,128)(2,1)S(1)}, bf16[512,512]{1,0:T(8,128)(2,1)}, u32[]{:S(2)}) copy-start(bf16[512,512]{1,0:T(8,128)(2,1)} %x_ref.1) | copy-start | bytes 1572868
  304.3 13.5 %all-to-all-start.2 = ((bf16[4,4,128,128]{3,2,1,0:T(8,128)(2,1)}), bf16[4,4,128,128]{3,2,1,0:T(8,128)(2,1)S(1)}, u32[]{:S(2)}, u32[]{:S(2)}) async-start(bf16[4,4,128,128]{3,2,1,0:T(8,128)(2,1)} %bitcast.5), calls=%async_computation.2 | async-start | bytes 1048576 | tf_op jit(solution)/shard_map/all_to_all | solution.py:201
Sparse Core Ops, SparseCore 0:
  31.5 36.0 all-gather.3

commit v2 on v1

--- a/solution.py
+++ b/solution.py
@@ -46,19 +46,139 @@
     )(x, wq, wk, wv)
 
 
-def attn_kernel(code_ref, q_ref, kv_hbm, o_ref, kv_ref, s_ref, sem):
-    chunks = 6
-    step = kv_hbm.shape[0] // chunks
-    copies = [
-        pltpu.make_async_copy(
-            kv_hbm.at[pl.ds(i * step, step)], kv_ref.at[pl.ds(i * step, step)], sem.at[i]
+MESH = pl.DeviceIdType.MESH
+DIRECT = 3
+UP_SET = (0, 2)
+DOWN_SET = (1, 3)
+
+
+def exchange_kernel(code_ref, q_ref, kv_ref, code_out, q_out, kv_out, transit, send_sem, recv_sem):
+    zone, dev = lax.axis_index("zone"), lax.axis_index("dev")
+    x, y_lo = zone // 2, zone % 2
+    y_hi, z, core = dev // 8, (dev // 2) % ZD, dev % 2
+    y = y_hi * 2 + y_lo
+
+    def at(px, py, pz, pc):
+        return (px * 2 + py % 2, (py // 2) * 8 + pz * 2 + pc)
+
+    side = 1 - 2 * y_lo
+    up, down = at(x, (y + 1) % 4, z, core), at(x, (y + 3) % 4, z, core)
+    halo, back = at((x + 4 + side) % 4, y, z, core), at((x + 4 - side) % 4, y, z, core)
+    partner = at(x, y, z, 1 - core)
+    z_at = [z] + [(z + d) % ZD for d in (1, 3, 2)]
+    z_dev = [None] + [at(x, y, z_at[j], core) for j in (1, 2, 3)]
+
+    barrier = pltpu.get_barrier_semaphore()
+    peers = [up, down, halo, back, partner] + z_dev[1:]
+    for peer in peers:
+        pl.semaphore_signal(barrier, inc=1, device_id=peer, device_id_type=MESH)
+    pl.semaphore_wait(barrier, len(peers))
+
+    live = []
+
+    def send(src, dst, target):
+        k = len(live)
+        copy = pltpu.make_async_remote_copy(
+            src_ref=src,
+            dst_ref=dst,
+            send_sem=send_sem.at[k],
+            recv_sem=recv_sem.at[k],
+            device_id=target,
+            device_id_type=MESH,
         )
-        for i in range(chunks)
-    ]
-    for c in copies:
-        c.start()
-    for c in copies:
-        c.wait()
+        copy.start()
+        live.append(copy)
+        return copy
+
+    def place(slot, j):
+        return kv_out.at[slot, core, z_at[j]]
+
+    kv_z, q_z, code_z, shared = {}, {}, {}, []
+    for j, lands in ((1, 2), (2, 1), (3, 3)):
+        kv_z[lands] = send(kv_ref.at[z_at[j]], kv_out.at[0, core, z], z_dev[j])
+    kv_out[0, core, z] = kv_ref[z]
+    q_out[z] = q_ref[z]
+    code_out[z] = code_ref[...]
+
+    from_up, from_down, far, halo_up, halo_down = {}, {}, {}, {}, {}
+
+    def spread_own(j, src):
+        from_down[j] = send(src, place(2, j), up)
+        from_up[j] = send(src, place(1, j), down)
+        if j == DIRECT:
+            from_down["x"] = send(src, transit, back)
+        shared.append(send(src, place(0, j), partner))
+
+    def pass_on(j):
+        from_up[j].wait_recv()
+        if j in DOWN_SET:
+            far[j] = send(place(1, j), place(3, j), down)
+        if j != DIRECT:
+            halo_up[j] = send(place(1, j), place(4, j), halo)
+        shared.append(send(place(1, j), place(1, j), partner))
+        from_down[j].wait_recv()
+        if j in UP_SET:
+            far[j] = send(place(2, j), place(3, j), up)
+        if j != DIRECT:
+            halo_down[j] = send(place(2, j), place(5, j), halo)
+        shared.append(send(place(2, j), place(2, j), partner))
+
+    spread_own(0, kv_ref.at[z])
+    for j, lands in ((1, 2), (2, 1), (3, 3)):
+        q_z[lands] = send(q_ref.at[z_at[j]], q_out.at[z], z_dev[j])
+        code_z[lands] = send(code_ref, code_out.at[z], z_dev[j])
+    for j in (1, 2):
+        kv_z[j].wait_recv()
+        spread_own(j, place(0, j))
+    pass_on(0)
+    kv_z[3].wait_recv()
+    spread_own(3, place(0, 3))
+    pass_on(1)
+    pass_on(2)
+    from_down["x"].wait_recv()
+    halo_down[DIRECT] = send(transit, place(5, DIRECT), up)
+    halo_up[DIRECT] = send(transit, place(4, DIRECT), down)
+    pass_on(3)
+    for j in range(4):
+        far[j].wait_recv()
+        shared.append(send(place(3, j), place(3, j), partner))
+        halo_up[j].wait_recv()
+        shared.append(send(place(4, j), place(4, j), partner))
+        halo_down[j].wait_recv()
+        shared.append(send(place(5, j), place(5, j), partner))
+    for c in shared + list(q_z.values()) + list(code_z.values()):
+        c.wait_recv()
+    for c in live:
+        c.wait_send()
+
+
+COPIES = 3 + 6 + 2 * 4 + 1 + 4 + 4 + 6 + 2 + 8 + 12
+
+
+def exchange(code, q, kv):
+    tiles = kv.shape[1]
+    piece = kv.shape[1:]
+    return pl.pallas_call(
+        exchange_kernel,
+        out_shape=(
+            jax.ShapeDtypeStruct((ZD,) + code.shape, jnp.int32),
+            jax.ShapeDtypeStruct(q.shape, q.dtype),
+            jax.ShapeDtypeStruct((6, 2, ZD) + piece, kv.dtype),
+        ),
+        in_specs=[pl.BlockSpec(memory_space=pltpu.VMEM)] * 3,
+        out_specs=[pl.BlockSpec(memory_space=pltpu.VMEM)] * 3,
+        scratch_shapes=[
+            pltpu.VMEM(piece, kv.dtype),
+            pltpu.SemaphoreType.DMA((COPIES,)),
+            pltpu.SemaphoreType.DMA((COPIES,)),
+        ],
+        compiler_params=pltpu.CompilerParams(
+            collective_id=0, has_side_effects=True, vmem_limit_bytes=24 * 1024 * 1024
+        ),
+    )(code, q, kv)
+
+
+def attn_kernel(code_ref, q_ref, kv_ref, o_ref, s_ref):
     lane = lax.broadcasted_iota(jnp.int32, (1, TILE), 1)
 
     def one_tile(i, carry):
@@ -118,15 +238,11 @@
         in_specs=[
             pl.BlockSpec(memory_space=pltpu.SMEM),
             pl.BlockSpec(memory_space=pltpu.VMEM),
-            pl.BlockSpec(memory_space=pl.ANY),
+            pl.BlockSpec(memory_space=pltpu.VMEM),
         ],
         out_specs=pl.BlockSpec(memory_space=pltpu.VMEM),
-        scratch_shapes=[
-            pltpu.VMEM(kv.shape, jnp.bfloat16),
-            pltpu.VMEM((4, TILE, 8 * TILE), jnp.float32),
-            pltpu.SemaphoreType.DMA((6,)),
-        ],
-        compiler_params=pltpu.CompilerParams(vmem_limit_bytes=40 * 1024 * 1024),
+        scratch_shapes=[pltpu.VMEM((4, TILE, 8 * TILE), jnp.float32)],
+        compiler_params=pltpu.CompilerParams(vmem_limit_bytes=24 * 1024 * 1024),
     )(code, q, kv)
 
 
@@ -145,20 +261,28 @@
 
 
 def make_codes(neighbour_blocks, neighbour_count, tile_valid, zone_blocks, zone_count):
-    zone_index = lax.axis_index("zone")
-    relative = (neighbour_blocks // zone_blocks - zone_index + 1) % zone_count
+    zone = lax.axis_index("zone")
+    y_lo = zone % 2
+    y = (lax.axis_index("dev") // 8) * 2 + y_lo
+    relative = (neighbour_blocks // zone_blocks - zone + 1) % zone_count
     local = neighbour_blocks % zone_blocks
     y_hi, rest = local // 32, local % 32
     z, rest = rest // 8, rest % 8
     core, t = rest // 4, rest % 4
-    slot = (((relative * 2 + y_hi) * 2 + core) * ZD + z) * 4 + t
+    other_y = y_hi * 2 + 1 - y_lo
+    above = (other_y - y + 4) % 4 == 1
+    same_x = relative == 2 - 2 * y_lo
+    near = jnp.where(same_x, jnp.where(above, 1, 2), jnp.where(above, 4, 5))
+    slot = jnp.where(relative == 1, jnp.where(y_hi == y // 2, 0, 3), near)
+    place = ((slot * 2 + core) * ZD + z) * 4 + t
     matches = neighbour_blocks[..., None] == jnp.arange(tile_valid.shape[0], dtype=jnp.int32)
     valid = jnp.sum(jnp.where(matches, tile_valid, 0), axis=-1)
     live = jnp.arange(NB, dtype=jnp.int32)[None, :] < neighbour_count[:, None]
-    code = slot * 256 + jnp.where(live, valid, 0)
-    return jnp.concatenate(
+    code = place * 256 + jnp.where(live, valid, 0)
+    code = jnp.concatenate(
         [code, neighbour_count[:, None], jnp.zeros((code.shape[0], 95), jnp.int32)], axis=1
     )
+    return jnp.concatenate([code, jnp.zeros_like(code)], axis=0)
 
 
 def body(
@@ -181,23 +305,16 @@
     z_groups = [
         [y * 8 + z * 2 + c for z in range(ZD)] for y in range(2) for c in range(2)
     ]
-    plane_groups = [
-        [y * 8 + z * 2 + c for y in range(2) for c in range(2)] for z in range(ZD)
-    ]
     codes = make_codes(
         neighbour_blocks, neighbour_count, tile_valid, tiles * dev_count, zone_count
     )
     q, kv = project(x, w_query, w_key, w_value)
-    codes = lax.all_gather(codes, "dev", axis=0, axis_index_groups=z_groups, tiled=True)
-    q = lax.all_to_all(q, "dev", 0, 0, axis_index_groups=z_groups, tiled=True)
-    kv = lax.all_to_all(kv, "dev", 0, 0, axis_index_groups=z_groups, tiled=True)
-    own = lax.all_gather(kv, "dev", axis=0, axis_index_groups=plane_groups)
-    own = own.reshape(dev_count * tiles, 2, TILE, HD)
-    ring = [(i, (i + 1) % zone_count) for i in range(zone_count)]
-    before = lax.ppermute(own, "zone", ring)
-    after = lax.ppermute(own, "zone", [(b, a) for a, b in ring])
-    near = jnp.concatenate([before, own, after], axis=0)
-    o = attend(codes, q.reshape(ZD * tiles, TILE, HD), near)
+    codes, q, kv = exchange(codes, q, kv)
+    o = attend(
+        codes[:, :tiles].reshape(ZD * tiles, -1),
+        q.reshape(ZD * tiles, TILE, HD),
+        kv.reshape(6 * 2 * ZD * tiles, 2, TILE, HD),
+    )
     o = lax.all_to_all(
         o.reshape(ZD, tiles, TILE, HD), "dev", 0, 0, axis_index_groups=z_groups, tiled=True
     )

time: 340 us -> 125 us (0.37)
  the two profiles are of different devices: /device:TPU:28 before, /device:TPU:16 now
where the time goes in v2:
time: 125 us; the launch traced here: 126 us
  Pallas kernels  92.3 us (74%)
  matrix products  12 us (10%)
  waiting for transfers between devices  9.34 us (7%)
  local copies, waits for them, and re-layouts  6.71 us (5%)
  starting transfers between devices  3.47 us (3%)
  other arithmetic  1.76 us (1%)
    pallas_call x1, Pallas kernels, exchange(): pl.pallas_call(exchange_kernel, out_shape=(jax.ShapeDtypeStruct((ZD,) + c...  51.1 us
    pallas_call x1, Pallas kernels, attend(): pl.pallas_call(attn_kernel, out_shape=jax.ShapeDtypeStruct(q.shape, jnp.b...  37.2 us
    all_to_all x1, waiting for transfers between devices, body(): lax.all_to_all(o.reshape(ZD, tiles, TILE, HD), 'dev', 0, 0, axis_index_gr...  9.34 us
    dot_general x1, matrix products, finish_layer(): jnp.dot(hidden, w_down, preferred_element_type=jnp.float32)  7.07 us
    pallas_call x1, Pallas kernels, project(): pl.pallas_call(proj_kernel, out_shape=(jax.ShapeDtypeStruct((HEADS, tiles...  4.05 us
    all_to_all x1, starting transfers between devices, body(): lax.all_to_all(o.reshape(ZD, tiles, TILE, HD), 'dev', 0, 0, axis_index_gr...  3.47 us
    unnamed x9, local copies, waits for them, and re-layouts  3.28 us
    dot_general x1, matrix products, finish_layer(): gate_part = jnp.dot(normed, w_gate, preferred_element_type=jnp.float32)  3.23 us
  transfers between devices with their start and end apart: 1, of which 1 were waited for; matrix products, arithmetic and copies ran while one was open for 1% of the time, Pallas kernels for 0%

profile of v2, /device:TPU:16, one launch (start us, length us, event | category | flops | bytes accessed | tf_op | source)
XLA Modules:
  0.0 125.7 jit_solution(17446338895717498597)
XLA Ops:
  0.0 0.0 copy-start
  0.0 0.9 copy.27
  0.9 0.1 pad.3.clone
  1.0 0.9 select_reduce_fusion
  1.9 0.8 select_add_fusion
  2.7 0.1 add_add_fusion
  2.7 4.0 %shard_map.109 = (bf16[4,4,128,128]{3,2,1,0:T(8,128)(2,1)}, bf16[4,4,2,128,128]{4,3,2,1,0:T(8,128)(2,1)}) custom-call(bf16[512,512]{1,0:T(8,128)(2,1)} %x_ref.1, bf16[512,512]{1,0:T(8,128)(2,1)} %wq_ref.1, bf16[512,512]{1,0:T(8,128)(2,1)} %wk_ref.1, bf16[512,512]{1,0:T(8,128)(2,1)} %wv_ref.1), custom_call_target="tpu_custom_call" | custom-call | tf_op jit(solution)/shard_map/pallas_call | solution.py:40
  6.8 0.0 copy-start.1
  6.8 1.2 copy-done.1
  8.0 0.0 copy-start.2
  8.0 1.0 copy-done.2
  9.1 51.1 %shard_map.110 = (s32[4,8,128]{2,1,0:T(8,128)S(1)}, bf16[4,4,128,128]{3,2,1,0:T(8,128)(2,1)S(1)}, bf16[6,2,4,4,2,128,128]{6,5,4,3,2,1,0:T(8,128)(2,1)S(1)}) custom-call(s32[8,128]{1,0:T(8,128)S(1)} %concatenate.7.code_ref, bf16[4,4,128,128]{3,2,1,0:T(8,128)(2,1)S(1)} %copy-done.2, bf16[4,4,2,128,128]{4,3,2,1,0:T(8,128)(2,1)S(1)} %copy-done.1), custom_call_target="tpu_custom_call" | custom-call | tf_op jit(solution)/shard_map/pallas_call | solution.py:161
  60.2 0.0 copy-start.3
  60.2 37.2 %shard_map.111 = bf16[16,128,128]{2,1,0:T(8,128)(2,1)} custom-call(s32[16,128]{1,0:T(8,128)S(1)} %bitcast.19, bf16[16,128,128]{2,1,0:T(8,128)(2,1)S(1)} %bitcast.18, bf16[192,2,128,128]{3,2,1,0:T(8,128)(2,1)S(1)} %bitcast.17), custom_call_target="tpu_custom_call" | custom-call | tf_op jit(solution)/shard_map/pallas_call | solution.py:235
  97.4 3.5 %all-to-all-start = ((bf16[4,4,128,128]{3,2,1,0:T(8,128)(2,1)}), bf16[4,4,128,128]{3,2,1,0:T(8,128)(2,1)S(1)}, u32[]{:S(2)}, u32[]{:S(2)}) async-start(bf16[4,4,128,128]{3,2,1,0:T(8,128)(2,1)} %bitcast.4), calls=%async_computation | async-start | bytes 1048576 | tf_op jit(solution)/shard_map/all_to_all | solution.py:318
  100.9 0.0 copy-done.3
  100.9 1.0 copy.26
  101.9 9.3 %all-to-all-done = bf16[4,4,128,128]{3,2,1,0:T(8,128)(2,1)S(1)} async-done(((bf16[4,4,128,128]{3,2,1,0:T(8,128)(2,1)}), bf16[4,4,128,128]{3,2,1,0:T(8,128)(2,1)S(1)}, u32[]{:S(2)}, u32[]{:S(2)}) %all-to-all-start) | async-done | bytes 524320 | tf_op jit(solution)/shard_map/all_to_all | solution.py:318
  111.2 0.4 copy.28
  111.6 1.7 %multiply_reduce_fusion = (f32[512]{0:T(512)S(1)}, f32[512,512]{0,1:T(8,128)S(1)}) fusion(bf16[512,512]{1,0:T(8,128)(2,1)} %param.18, bf16[64,8,4,128]{3,2,1,0:T(4,128)(2,1)S(1)} %bitcast.21, bf16[512,512]{0,1:T(8,128)(2,1)} %copy.26), kind=kOutput, calls=%fused_computation.6 | convolution fusion | flops 269483520 | bytes 2623488 | tf_op jit(solution)/shard_map/dot_general | solution.py:250
  113.4 0.0 copy-done
  113.4 3.2 %fusion.3 = f32[512,2048]{1,0:T(8,128)} fusion(bf16[512,2048]{1,0:T(8,128)(2,1)S(1)} %copy-done, f32[512,512]{0,1:T(8,128)S(1)} %get-tuple-element.16, f32[512]{0:T(512)S(1)} %add_rsqrt_fusion), kind=kOutput, calls=%fused_computation.7 | convolution fusion | flops 1074266112 | bytes 7342080 | tf_op jit(solution)/shard_map/dot_general | solution.py:255
  116.6 7.1 %fusion.2 = bf16[512,512]{0,1:T(8,128)(2,1)} fusion(f32[512,512]{0,1:T(8,128)S(1)} %get-tuple-element.16, bf16[2048,512]{1,0:T(8,128)(2,1)} %param.21, f32[512,2048]{1,0:T(8,128)} %fusion.3, bf16[512,2048]{1,0:T(8,128)(2,1)} %param.20, f32[512]{0:T(512)S(1)} %add_rsqrt_fusion), kind=kOutput, calls=%fused_computation.4 | convolution fusion | flops 2154823680 | bytes 9963520 | tf_op jit(solution)/shard_map/dot_general | solution.py:258
  123.7 2.0 %copy.30 = bf16[512,512]{1,0:T(8,128)(2,1)} copy(bf16[512,512]{0,1:T(8,128)(2,1)} %fusion.2) | data formatting | bytes 1048576 | tf_op jit(solution)/shard_map/convert_element_type | solution.py:258
  (4 shorter events, 0.0 us)
Async XLA Ops:
  0.0 113.4 %copy-start = (bf16[512,2048]{1,0:T(8,128)(2,1)S(1)}, bf16[512,2048]{1,0:T(8,128)(2,1)}, u32[]{:S(2)}) copy-start(bf16[512,2048]{1,0:T(8,128)(2,1)} %param.19) | copy-start | bytes 6291460
  6.8 1.2 copy-start.1
  8.0 1.0 copy-start.2
  60.2 40.7 %copy-start.3 = (bf16[512,512]{1,0:T(8,128)(2,1)S(1)}, bf16[512,512]{1,0:T(8,128)(2,1)}, u32[]{:S(2)}) copy-start(bf16[512,512]{1,0:T(8,128)(2,1)} %x_ref.1) | copy-start | bytes 1572868
  97.4 13.8 %all-to-all-start = ((bf16[4,4,128,128]{3,2,1,0:T(8,128)(2,1)}), bf16[4,4,128,128]{3,2,1,0:T(8,128)(2,1)S(1)}, u32[]{:S(2)}, u32[]{:S(2)}) async-start(bf16[4,4,128,128]{3,2,1,0:T(8,128)(2,1)} %bitcast.4), calls=%async_computation | async-start | bytes 1048576 | tf_op jit(solution)/shard_map/all_to_all | solution.py:318
